TPU v7x, 32 devices: a whole 2x2x4 slice. The times are simulated.
32 devices in a mesh: grp: 4 (over x, core), dp: 4 (over z), seq: 2 (over y).
Axes of the slice: x: 2, y: 2, z: 4, core: 2. Of those that a mesh axis runs over, the one named last changes fastest.
Arguments:
- student_saved_input: bfloat16 [16, 256, 3584], P(('grp', 'dp'), 'seq'), may hold values from -6 to 6
- student_saved_query: bfloat16 [16, 256, 1792], P(('grp', 'dp'), 'seq'), may hold values from -600 to 600
- feature_cotangent: bfloat16 [16, 256, 1792], P(('grp', 'dp'), 'seq'), may hold values from -6 to 6
- feature_weights: bfloat16 [128, 896], replicated, may hold values from -0.5 to 0.5
- adapter_down_weight: bfloat16 [8, 3584], replicated, may hold values from -0.09375 to 0.09375
- adapter_up_weight: bfloat16 [8, 1792], replicated, may hold values from -0.09375 to 0.09375
- teacher_next_query: bfloat16 [16, 512, 1792], P(('grp', 'dp'), 'seq'), may hold values from -6 to 6
- teacher_next_key: bfloat16 [16, 512, 256], P(('grp', 'dp'), 'seq'), may hold values from -6 to 6
- teacher_next_value: bfloat16 [16, 512, 256], P(('grp', 'dp'), 'seq'), may hold values from -6 to 6
- positions: int32 [16, 512], P(('grp', 'dp'), 'seq'), may hold values from 0 to 511, each once within a row
Outputs:
- teacher_output: bfloat16 [16, 512, 1792], P(('grp', 'dp'), 'seq')
- grad_feature: float32 [128, 896], P('dp')
- grad_down: float32 [8, 3584], P(None, 'dp')
- up_gradient: float32 [8, 1792], P(None, 'dp')
Inputs may be any that keep to these rules, and one draw needn't show every extreme that they name: `positions`: each sequence's row is a permutation of 0 to 511.
All inputs are finite; a program needn't handle non-finite values.
Results may differ from a plain program's by a relative error of at most 0.015.
Values may be sent and summed in bfloat16 or wider, within the bound.
A program may use at most 64 MiB of HBM per device.

v0:
```python
import jax
import jax.numpy as jnp
from jax import lax
from jax.sharding import PartitionSpec as P

HEAD_SIZE = 128
F = 64


adapter_scale = 2.0
masked_score = -1e30
key_block = 512


def student_gradients(
    student_saved_input,
    student_saved_query,
    feature_cotangent,
    feature_weights,
    adapter_down_weight,
    adapter_up_weight,
):
    row_count = student_saved_query.shape[0] * student_saved_query.shape[1]
    head_count = feature_weights.shape[1] // F
    heads_of_queries = student_saved_query.reshape(row_count, head_count, HEAD_SIZE)
    map_heads = feature_weights.reshape(HEAD_SIZE, head_count, F)
    logits = jnp.einsum(
        "shd,dhf->shf", heads_of_queries, map_heads, preferred_element_type=jnp.float32
    )
    prob_plus = jax.nn.softmax(logits, axis=-1)
    prob_minus = jax.nn.softmax(-logits, axis=-1)
    cotangent = feature_cotangent.reshape(row_count, head_count, 2 * F).astype(jnp.float32)
    cot_plus = cotangent[..., :F]
    cot_minus = cotangent[..., F:]
    dlogit = prob_plus * (
        cot_plus - jnp.sum(prob_plus * cot_plus, axis=-1, keepdims=True)
    ) - prob_minus * (cot_minus - jnp.sum(prob_minus * cot_minus, axis=-1, keepdims=True))
    dlogit_b = dlogit.astype(jnp.bfloat16)
    grad_map = jnp.einsum(
        "shd,shf->dhf", heads_of_queries, dlogit_b, preferred_element_type=jnp.float32
    ).reshape(HEAD_SIZE, head_count * F)
    query_gradient = (
        jnp.einsum("shf,dhf->shd", dlogit_b, map_heads, preferred_element_type=jnp.float32)
        .reshape(row_count, head_count * HEAD_SIZE)
        .astype(jnp.bfloat16)
    )
    input_rows = student_saved_input.reshape(row_count, -1)
    down_activation = jnp.dot(
        input_rows, adapter_down_weight.T, preferred_element_type=jnp.float32
    ).astype(jnp.bfloat16)
    up_gradient = adapter_scale * jnp.dot(
        down_activation.T, query_gradient, preferred_element_type=jnp.float32
    )
    lowrank_gradient = (
        adapter_scale
        * jnp.dot(query_gradient, adapter_up_weight.T, preferred_element_type=jnp.float32)
    ).astype(jnp.bfloat16)
    grad_down = jnp.dot(lowrank_gradient.T, input_rows, preferred_element_type=jnp.float32)
    return (grad_map, grad_down, up_gradient)


def reduce_grads(grads):
    along_seq = (
        lax.psum(grads[0].astype(jnp.bfloat16), "seq").astype(jnp.float32),
        lax.psum(grads[1].astype(jnp.bfloat16), "seq").astype(jnp.float32),
        lax.psum(grads[2].astype(jnp.bfloat16), "seq").astype(jnp.float32),
    )
    shards = (
        lax.psum_scatter(
            along_seq[0].astype(jnp.bfloat16), "dp", scatter_dimension=0, tiled=True
        ).astype(jnp.float32),
        lax.psum_scatter(
            along_seq[1].astype(jnp.bfloat16), "dp", scatter_dimension=1, tiled=True
        ).astype(jnp.float32),
        lax.psum_scatter(
            along_seq[2].astype(jnp.bfloat16), "dp", scatter_dimension=1, tiled=True
        ).astype(jnp.float32),
    )
    return (
        lax.psum(shards[0].astype(jnp.bfloat16), "grp").astype(jnp.float32),
        lax.psum(shards[1].astype(jnp.bfloat16), "grp").astype(jnp.float32),
        lax.psum(shards[2].astype(jnp.bfloat16), "grp").astype(jnp.float32),
    )


def teacher_attention(teacher_next_query, teacher_next_key, teacher_next_value, positions):
    query_count = teacher_next_query.shape[1]
    kv_heads = teacher_next_key.shape[2] // HEAD_SIZE
    group_width = teacher_next_query.shape[2] // HEAD_SIZE // kv_heads
    heads_of_queries = teacher_next_query[0].reshape(query_count, kv_heads, group_width, HEAD_SIZE)
    query_pos = positions[0]
    scale_factor = HEAD_SIZE ** (-0.5)

    def one_block(state, rows_of_keys, rows_of_values, key_pos):
        running_max, denom, accum = state
        score = (
            jnp.einsum(
                "qcgd,kcd->cgqk", heads_of_queries, rows_of_keys, preferred_element_type=jnp.float32
            )
            * scale_factor
        )
        allowed = (key_pos[None, :] <= query_pos[:, None])[None, None]
        score = jnp.where(allowed, score, masked_score)
        new_max = jnp.maximum(running_max, jnp.max(score, axis=-1))
        factor = jnp.exp(running_max - new_max)
        weights = jnp.where(allowed, jnp.exp(score - new_max[..., None]), 0.0)
        denom = denom * factor + jnp.sum(weights, axis=-1)
        update = jnp.einsum(
            "cgqk,kcd->qcgd",
            weights.astype(jnp.bfloat16),
            rows_of_values,
            preferred_element_type=jnp.float32,
        )
        accum = accum * jnp.transpose(factor, (2, 0, 1))[..., None] + update
        return (new_max, denom, accum)

    start_state = (
        jnp.full((kv_heads, group_width, query_count), masked_score, jnp.float32),
        jnp.zeros((kv_heads, group_width, query_count), jnp.float32),
        jnp.zeros((query_count, kv_heads, group_width, HEAD_SIZE), jnp.float32),
    )
    key_piece = lax.all_gather(teacher_next_key, "seq", axis=1, tiled=True)
    value_piece = lax.all_gather(teacher_next_value, "seq", axis=1, tiled=True)
    pos_piece = lax.all_gather(positions, "seq", axis=1, tiled=True)
    piece_rows = key_piece.shape[1]
    keys_all = key_piece[0].reshape(piece_rows, kv_heads, HEAD_SIZE)
    values_all = value_piece[0].reshape(piece_rows, kv_heads, HEAD_SIZE)
    pos_all = pos_piece[0]

    def advance(index, inner):
        begin = index * key_block
        return one_block(
            inner,
            lax.dynamic_slice_in_dim(keys_all, begin, key_block, 0),
            lax.dynamic_slice_in_dim(values_all, begin, key_block, 0),
            lax.dynamic_slice_in_dim(pos_all, begin, key_block, 0),
        )

    running_max, denom, accum = lax.fori_loop(0, piece_rows // key_block, advance, start_state)
    output = accum / jnp.transpose(denom, (2, 0, 1))[..., None]
    return output.astype(jnp.bfloat16).reshape(1, query_count, -1)


def on_device(
    student_saved_input,
    student_saved_query,
    feature_cotangent,
    feature_weights,
    adapter_down_weight,
    adapter_up_weight,
    teacher_next_query,
    teacher_next_key,
    teacher_next_value,
    positions,
):
    teacher_output = teacher_attention(
        teacher_next_query, teacher_next_key, teacher_next_value, positions
    )
    grads = student_gradients(
        student_saved_input,
        student_saved_query,
        feature_cotangent,
        feature_weights,
        adapter_down_weight,
        adapter_up_weight,
    )
    grad_feature, grad_down, up_gradient = reduce_grads(grads)
    return (teacher_output, grad_feature, grad_down, up_gradient)


def solution(mesh):
    placed = (
        P(("grp", "dp"), "seq", None),
        P(("grp", "dp"), "seq", None),
        P(("grp", "dp"), "seq", None),
        P(),
        P(),
        P(),
        P(("grp", "dp"), "seq", None),
        P(("grp", "dp"), "seq", None),
        P(("grp", "dp"), "seq", None),
        P(("grp", "dp"), "seq"),
    )
    return jax.shard_map(
        on_device,
        mesh=mesh,
        in_specs=placed,
        out_specs=(P(("grp", "dp"), "seq", None), P("dp", None), P(None, "dp"), P(None, "dp")),
        check_vma=False,
    )
```

profile of v0, /device:TPU:0, one launch (start us, length us, event | category | flops | bytes accessed | tf_op | source)
XLA Modules:
  0.0 152.9 jit_solution(6718897974709875448)
XLA Ops:
  7.2 1.3 copy.44
  11.1 1.2 copy.46
  12.8 1.5 convolution_convert_fusion.1
  16.6 1.3 copy.58
  17.9 1.6 %convolution_convert_fusion.2 = bf16[14,64,128]{2,1,0:T(8,128)(2,1)S(1)} fusion(bf16[128,14,128]{0,2,1:T(8,128)(2,1)S(1)} %bitcast.93, f32[128,14,64]{0,2,1:T(8,128)S(1)} %fusion.27, f32[128,14,64]{0,2,1:T(8,128)} %fusion.18, f32[128,14,128]{0,2,1:T(8,128)S(1)} %bitcast.89), kind=kOutput, calls=%fused_computation.33 | convolution fusion | flops 30050112 | bytes 2981888 | tf_op jit(solution)/shard_map/shd,shf->dhf/dot_general | solution.py:39
  20.4 5.2 %all_gather.11 = s32[1,512]{1,0:T(1,128)S(1)} all-gather(s32[1,256]{1,0:T(1,128)S(1)} %copy-done.6), channel_id=1, replica_groups=mesh['grp'=4,'dp'=4,'seq'=2] {'seq'}, dimensions={1}, use_global_device_ids=true | all-gather | bytes 3072 | tf_op jit(solution)/shard_map/all_gather | solution.py:124
  25.6 1.5 copy.38
  27.2 5.6 %all_gather.13 = bf16[1,512,256]{1,2,0:T(8,128)(2,1)S(1)} all-gather(bf16[1,256,256]{1,2,0:T(8,128)(2,1)S(1)} %copy.37), channel_id=1, replica_groups=mesh['grp'=4,'dp'=4,'seq'=2] {'seq'}, dimensions={1}, use_global_device_ids=true | all-gather | bytes 393216 | tf_op jit(solution)/shard_map/all_gather | solution.py:122
  33.0 1.3 fusion.6
  34.4 2.9 %copy-done.1 = f32[2,512,256,7]{2,1,3,0:T(8,128)} copy-done((f32[2,512,256,7]{2,1,3,0:T(8,128)}, f32[2,512,256,7]{2,1,3,0:T(8,128)S(1)}, u32[]{:S(2)}) %copy-start.1) | copy-done | bytes 7340056
  37.3 1.8 %fusion.7 = f32[2,7,256]{2,1,0:T(8,128)S(1)} fusion(f32[2,512,256,7]{2,1,3,0:T(8,128)S(1)} %get-tuple-element.55, f32[2,7,256]{2,1,0:T(8,128)S(1)} %get-tuple-element.53, pred[256,512]{0,1:T(8,128)(4,1)S(1)} %broadcast_compare_fusion), kind=kLoop, calls=%fused_computation.9 | loop fusion | flops 9171456 | bytes 7499776 | tf_op jit(solution)/shard_map/while/body/eval_jaxpr/reduce_sum | solution.py:107
  39.2 1.2 reduce-scatter.12.cloned.1.call-done
  40.4 1.6 %copy.61 = bf16[8,448]{1,0:T(8,128)(2,1)} copy(bf16[8,448]{0,1:T(8,128)(2,1)} %bitcast.102) | data formatting | bytes 14336
  42.0 24.8 %reduce-scatter.10.cloned.1.call-done = bf16[896,8]{1,0:T(8,128)(2,1)} async-done(((bf16[3584,8]{1,0:T(8,128)(2,1)}), bf16[896,8]{1,0:T(8,128)(2,1)}) %reduce-scatter.10.cloned.1.call-update) | async-done | bytes 14352
  66.7 1.6 %copy.59 = bf16[8,896]{1,0:T(8,128)(2,1)} copy(bf16[8,896]{0,1:T(8,128)(2,1)} %bitcast.101) | data formatting | bytes 28672
  68.4 19.4 %reduce-scatter.8.cloned.1.call-done = bf16[32,896]{1,0:T(8,128)(2,1)} async-done(((bf16[128,896]{1,0:T(8,128)(2,1)}), bf16[32,896]{1,0:T(8,128)(2,1)}) %reduce-scatter.8.cloned.1.call-update) | async-done | bytes 57360 | tf_op jit(solution)/shard_map/reduce_scatter | solution.py:69
  87.9 5.6 %all_gather.14 = bf16[1,512,256]{2,1,0:T(8,128)(2,1)S(1)} all-gather(bf16[1,256,256]{2,1,0:T(8,128)(2,1)S(1)} %copy-done.2), channel_id=1, replica_groups=mesh['grp'=4,'dp'=4,'seq'=2] {'seq'}, dimensions={1}, use_global_device_ids=true | all-gather | bytes 393216 | tf_op jit(solution)/shard_map/all_gather | solution.py:123
  93.6 16.4 %all-reduce.7.cloned.1.call-done = (bf16[32,896]{1,0:T(8,128)(2,1)}, bf16[8,896]{1,0:T(8,128)(2,1)}, bf16[8,448]{1,0:T(8,128)(2,1)}) async-done(((bf16[32,896]{1,0:T(8,128)(2,1)}, bf16[8,896]{1,0:T(8,128)(2,1)}, bf16[8,448]{1,0:T(8,128)(2,1)}), (bf16[32,896]{1,0:T(8,128)(2,1)}, bf16[8,896]{1,0:T(8,128)(2,1)}, bf16[8,448]{1,0:T(8,128)(2,1)})) %all-reduce.7.cloned.1.call-update) | async-done | bytes 78864 | tf_op jit(solution)/shard_map/psum | solution.py:64
  110.1 5.2 %fusion.14 = bf16[256,2,7,128]{0,3,2,1:T(8,128)(2,1)S(1)} fusion(bf16[512,2,128,1]{0,2,3,1:T(8,128)(2,1)S(1)} %bitcast.100, f32[2,512,256,7]{2,1,3,0:T(8,128)} %copy-done.1, f32[2,7,256]{2,1,0:T(8,128)S(1)} %get-tuple-element.53, pred[256,512]{0,1:T(8,128)(4,1)S(1)} %broadcast_compare_fusion, f32[256,2,7]{0,2,1:T(8,128)S(1)} %bitcast_add_fusion.1, ...), kind=kOutput, calls=%fused_computation.18 | convolution fusion | flops 480313344 | bytes 8693760 | tf_op jit(solution)/shard_map/while/body/eval_jaxpr/cgqk,kcd->qcgd/dot_general | solution.py:108
  115.3 1.4 copy.49
  116.6 25.7 %all-reduce.5.cloned.1.call-done = (bf16[32,896]{1,0:T(8,128)(2,1)}, bf16[8,896]{1,0:T(8,128)(2,1)}, bf16[8,448]{1,0:T(8,128)(2,1)}) async-done(((bf16[32,896]{1,0:T(8,128)(2,1)}, bf16[8,896]{1,0:T(8,128)(2,1)}, bf16[8,448]{1,0:T(8,128)(2,1)}), (bf16[32,896]{1,0:T(8,128)(2,1)}, bf16[8,896]{1,0:T(8,128)(2,1)}, bf16[8,448]{1,0:T(8,128)(2,1)})) %all-reduce.5.cloned.1.call-update) | async-done | bytes 78864 | tf_op jit(solution)/shard_map/psum | solution.py:80
  142.3 1.5 convert_element_type.75
  143.8 1.3 convert_element_type.81
  145.1 1.3 convert_element_type.84
  (36 shorter events, 6.7 us)
Async XLA Ops:
  7.2 7.2 %copy-start = (bf16[1,128,3584]{2,1,0:T(8,128)(2,1)S(1)}, bf16[1,128,3584]{2,1,0:T(8,128)(2,1)}, u32[]{:S(2)}) copy-start(bf16[1,128,3584]{2,1,0:T(8,128)(2,1)} %param.10) | copy-start | bytes 2752516
  7.2 7.2 %copy-start.4 = (bf16[8,3584]{1,0:T(8,128)(2,1)S(1)}, bf16[8,3584]{1,0:T(8,128)(2,1)}, u32[]{:S(2)}) copy-start(bf16[8,3584]{1,0:T(8,128)(2,1)} %param.14) | copy-start | bytes 172036
  7.2 9.0 %copy-start.5 = (bf16[8,1792]{1,0:T(8,128)(2,1)S(1)}, bf16[8,1792]{1,0:T(8,128)(2,1)}, u32[]{:S(2)}) copy-start(bf16[8,1792]{1,0:T(8,128)(2,1)} %param.15) | copy-start | bytes 86020
  7.2 33.2 %reduce-scatter.12.cloned.1.call-start = ((), (), s32[]{:S(2)}) async-start(), calls=%async_computation.5 | async-start | bytes 573440
  10.0 10.4 %copy-start.6 = (s32[1,256]{1,0:T(1,128)S(1)}, s32[1,256]{1,0:T(1,128)}, u32[]{:S(2)}) copy-start(s32[1,256]{1,0:T(1,128)} %param.19) | copy-start | bytes 3076
  14.3 12.8 %copy-start.3 = (bf16[1,256,256]{2,1,0:T(8,128)(2,1)S(1)}, bf16[1,256,256]{2,1,0:T(8,128)(2,1)}, u32[]{:S(2)}) copy-start(bf16[1,256,256]{2,1,0:T(8,128)(2,1)} %param.17) | copy-start | bytes 393220
  16.2 50.6 %reduce-scatter.10.cloned.1.call-start = ((), (), s32[]{:S(2)}) async-start(), calls=%async_computation.4 | async-start | bytes 1146880
  17.9 69.9 %reduce-scatter.8.cloned.1.call-start = ((), (), s32[]{:S(2)}) async-start(), calls=%async_computation.3 | async-start | bytes 286720 | tf_op jit(solution)/shard_map/reduce_scatter | solution.py:69
  20.4 89.7 %all-reduce.7.cloned.1.call-start = ((), (), s32[]{:S(2)}) async-start(), calls=%async_computation.7 | async-start | bytes 159744 | tf_op jit(solution)/shard_map/psum | solution.py:64
  33.0 54.8 %copy-start.2 = (bf16[1,256,256]{2,1,0:T(8,128)(2,1)S(1)}, bf16[1,256,256]{2,1,0:T(8,128)(2,1)}, u32[]{:S(2)}) copy-start(bf16[1,256,256]{2,1,0:T(8,128)(2,1)} %param.18) | copy-start | bytes 393220
  34.4 3.0 %copy-start.1 = (f32[2,512,256,7]{2,1,3,0:T(8,128)}, f32[2,512,256,7]{2,1,3,0:T(8,128)S(1)}, u32[]{:S(2)}) copy-start(f32[2,512,256,7]{2,1,3,0:T(8,128)S(1)} %get-tuple-element.55) | copy-start | bytes 22020100
  87.8 54.5 %all-reduce.5.cloned.1.call-start = ((), (), s32[]{:S(2)}) async-start(), calls=%async_computation.6 | async-start | bytes 159744 | tf_op jit(solution)/shard_map/psum | solution.py:80
Sparse Core Ops, SparseCore 0:
  16.3 24.0 reduce-scatter.11
  43.3 23.4 reduce-scatter.9
  69.0 18.6 reduce-scatter.7
  90.6 19.4 all-reduce.6
  112.4 29.8 all-reduce.4
where the time goes:
time: 153 us
  waiting for transfers between devices  87.6 us (57%)
  blocking collectives  16.5 us (11%)
  local copies, waits for them, and re-layouts  16 us (10%)
  between operations  14 us (9%)
  matrix products  12.1 us (8%)
  other arithmetic  6.57 us (4%)
    unnamed x7, waiting for transfers between devices  26.1 us
    psum x1, waiting for transfers between devices, reduce_grads(): lax.psum(shards[0].astype(jnp.bfloat16), 'grp').astype(jnp.float32)  25.7 us
    reduce_scatter x1, waiting for transfers between devices, reduce_grads(): lax.psum_scatter(along_seq[0].astype(jnp.bfloat16), 'dp', scatter_dimensi...  19.4 us
    psum x1, waiting for transfers between devices, reduce_grads(): lax.psum(grads[0].astype(jnp.bfloat16), 'seq').astype(jnp.float32)  16.4 us
    unnamed x23, local copies, waits for them, and re-layouts  13.8 us
    all_gather x1, blocking collectives, teacher_attention(): key_piece = lax.all_gather(teacher_next_key, 'seq', axis=1, tiled=True)  5.65 us
    all_gather x1, blocking collectives, teacher_attention(): value_piece = lax.all_gather(teacher_next_value, 'seq', axis=1, tiled=True)  5.64 us
    all_gather x1, blocking collectives, teacher_attention(): pos_piece = lax.all_gather(positions, 'seq', axis=1, tiled=True)  5.2 us
  transfers between devices with their start and end apart: 5, of which 5 were waited for; matrix products, arithmetic and copies ran while one was open for 12% of the time, Pallas kernels for 0%

commit v1 on v0

v1 whole, which is shorter than its diff:
```python
import functools

import jax
import jax.numpy as jnp
from jax import lax
from jax.experimental import pallas as pl
from jax.experimental.pallas import tpu as pltpu
from jax.sharding import PartitionSpec as P

MESH = pl.DeviceIdType.MESH
HEAD_SIZE = 128
F = 64
LANES = 128
ROWS = 8
ADAPTER_SCALE = 2.0
MASKED = -1e30
LOG2E = 1.4426950408889634
BF16 = jnp.bfloat16
F32 = jnp.float32


def dot(a, b, dims=((1,), (0,))):
    return lax.dot_general(a, b, (dims, ((), ())), preferred_element_type=F32)


class Plan:
    def __init__(self, n_grp, n_dp, n_seq, feature_shape, down_width, up_width):
        self.n_grp, self.n_dp, self.n_seq = n_grp, n_dp, n_seq
        self.plane = n_grp // 2 * n_seq
        self.feature_rows = feature_shape[0] // n_dp
        self.down_width, self.up_width = down_width // n_dp, up_width // n_dp
        halves = []
        pairs = max(1, self.feature_rows // 16)
        for block in range(pairs):
            for tile in range(feature_shape[1] // LANES):
                for row in range(block * 16, min(block * 16 + 16, self.feature_rows), ROWS):
                    halves.append((0, row, tile * LANES, LANES))
        for which, width in ((1, self.down_width), (2, self.up_width)):
            for begin in range(0, width, LANES):
                halves.append((which, 0, begin, min(LANES, width - begin)))
        self.halves = halves
        self.used = (len(halves) + 1) // 2
        step = 2 * self.plane
        self.per = -(-self.used // step)
        self.units = self.per * step

    def where(self, unit):
        core, rest = divmod(unit, self.plane * self.per)
        return (core,) + divmod(rest, self.per)


def kernel(
    plan,
    x_hbm, sq_hbm, cot_hbm, w_hbm, ad_hbm, au_hbm, tq_hbm, tk_hbm, tv_hbm, pos_hbm,
    out_ref, gf_out, gd_out, gu_out,
    x_ref, sq_ref, cot_ref, w_ref, ad_ref, au_ref, tq_ref, k_ref, v_ref, pos_ref,
    bias_ref, dq_ref, gf_ref, gd_ref, gu_ref,
    g_ref, r1_ref, s1_ref, r2_ref, s2_ref, r3_ref, a_ref,
    load_sem, kv_send, kv_recv, core_send, core_recv, plane_send, plane_recv,
    dp_send, dp_recv, all_send, all_recv,
):
    n_dp, n_seq, n_grp, n_plane, per = plan.n_dp, plan.n_seq, plan.n_grp, plan.plane, plan.per
    grp, dp, seq = lax.axis_index("grp"), lax.axis_index("dp"), lax.axis_index("seq")
    core = lax.rem(grp, 2)
    mine = lax.div(grp, 2) * n_seq + seq

    def in_plane(index, which_core):
        return {"grp": lax.div(index, n_seq) * 2 + which_core, "dp": dp, "seq": lax.rem(index, n_seq)}

    loads = []
    for n, (src, dst) in enumerate(
        (
            (pos_hbm, pos_ref.at[0]), (tk_hbm.at[0], k_ref.at[0]), (tv_hbm.at[0], v_ref.at[0]),
            (w_hbm, w_ref), (sq_hbm.at[0], sq_ref), (cot_hbm.at[0], cot_ref), (ad_hbm, ad_ref),
            (x_hbm.at[0], x_ref), (au_hbm, au_ref), (tq_hbm.at[0], tq_ref),
        )
    ):
        copy = pltpu.make_async_copy(src, dst, load_sem.at[n])
        copy.start()
        loads.append(copy)

    barrier = pltpu.get_barrier_semaphore()
    greeted = 0
    for j in range(1, n_plane):
        for other in range(2):
            pl.semaphore_signal(
                barrier, inc=1, device_id=in_plane(lax.rem(mine + j, n_plane), other), device_id_type=MESH
            )
            greeted += 1
    partner = {"grp": grp + 1 - 2 * core, "dp": dp, "seq": seq}
    pl.semaphore_signal(barrier, inc=1, device_id=partner, device_id_type=MESH)
    for j in range(1, n_dp):
        pl.semaphore_signal(
            barrier, inc=1, device_id={"grp": grp, "dp": lax.rem(dp + j, n_dp), "seq": seq}, device_id_type=MESH
        )
    greeted += n_dp

    for unit in range(plan.used, plan.units):
        c, p, k = plan.where(unit)
        g_ref[c, p, :, k] = jnp.zeros((n_dp, 16, LANES), BF16)

    for n in range(3):
        loads[n].wait()
    pl.semaphore_wait(barrier, greeted)

    kv_copies = []
    for n, ref in enumerate((pos_ref, k_ref, v_ref)):
        for j in range(1, n_seq):
            copy = pltpu.make_async_remote_copy(
                src_ref=ref.at[0], dst_ref=ref.at[j],
                send_sem=kv_send.at[n, j], recv_sem=kv_recv.at[n, j],
                device_id={"grp": grp, "dp": dp, "seq": lax.rem(seq + j, n_seq)}, device_id_type=MESH,
            )
            copy.start()
            kv_copies.append(copy)

    rows = sq_ref.shape[0]
    lane = lax.broadcasted_iota(jnp.int32, (rows, LANES), 1)
    first = lane < F
    wide = lax.broadcasted_iota(jnp.int32, (2 * LANES, LANES), 1) < F
    depth = lax.broadcasted_iota(jnp.int32, (2 * LANES, LANES), 0)
    ones = ((lax.rem(depth, LANES) < F) == wide).astype(F32).astype(BF16)
    w_half = lax.broadcasted_iota(jnp.int32, (HEAD_SIZE, LANES), 1) < F

    def half_max(values):
        one = jnp.max(jnp.where(first, values, -jnp.inf), axis=1, keepdims=True)
        two = jnp.max(jnp.where(first, -jnp.inf, values), axis=1, keepdims=True)
        return jnp.where(first, one, two)

    def half_sum(values):
        stack = jnp.concatenate(values, axis=0)
        high = stack.astype(BF16)
        low = (stack - high.astype(F32)).astype(BF16)
        sums = dot(jnp.concatenate([high, low], axis=1), ones)
        return [sums[n * rows:(n + 1) * rows] for n in range(len(values))]

    for n in range(3, 6):
        loads[n].wait()
    for j in range(w_ref.shape[1] // LANES):
        q2 = sq_ref[:, 2 * LANES * j:2 * LANES * (j + 1)]
        w = w_ref[:, LANES * j:LANES * (j + 1)].astype(F32)
        w2 = jnp.concatenate([jnp.where(w_half, w, 0.0), jnp.where(w_half, 0.0, w)], axis=0).astype(BF16)
        logit = dot(q2, w2)
        plus = jnp.exp(logit - half_max(logit))
        minus = jnp.exp(-logit - half_max(-logit))
        cot_a = cot_ref[:, 2 * LANES * j:2 * LANES * j + LANES].astype(F32)
        cot_b = cot_ref[:, 2 * LANES * j + LANES:2 * LANES * (j + 1)].astype(F32)
        cot_plus = jnp.where(first, cot_a, pltpu.roll(cot_b, F, 1))
        cot_minus = jnp.where(first, pltpu.roll(cot_a, F, 1), cot_b)
        sum_p, sum_m, sum_pc, sum_mc = half_sum([plus, minus, plus * cot_plus, minus * cot_minus])
        inv_p, inv_m = 1.0 / sum_p, 1.0 / sum_m
        dlogit = plus * inv_p * (cot_plus - sum_pc * inv_p) - minus * inv_m * (cot_minus - sum_mc * inv_m)
        dlogit_b = dlogit.astype(BF16)
        grad = dot(q2, dlogit_b, ((0,), (0,)))
        gf_ref[:, LANES * j:LANES * (j + 1)] = jnp.where(w_half, grad[:HEAD_SIZE], grad[HEAD_SIZE:])
        dq_ref[:, 2 * LANES * j:2 * LANES * (j + 1)] = dot(dlogit_b, w2, ((1,), (1,))).astype(BF16)
    for n in range(6, 9):
        loads[n].wait()
    down_act = dot(ad_ref[...], x_ref[...], ((1,), (1,))).astype(BF16)
    gu_ref[...] = ADAPTER_SCALE * dot(down_act, dq_ref[...])
    dlow = (ADAPTER_SCALE * dot(au_ref[...], dq_ref[...], ((1,), (1,)))).astype(BF16)
    gd_ref[...] = dot(dlow, x_ref[...])

    def half_unit(index, d):
        if index >= len(plan.halves):
            return jnp.zeros((ROWS, LANES), F32)
        which, row, begin, width = plan.halves[index]
        if which == 0:
            row = d * plan.feature_rows + row
            return gf_ref[row:row + ROWS, begin:begin + LANES]
        ref, own = ((gd_ref, plan.down_width), (gu_ref, plan.up_width))[which - 1]
        begin = d * own + begin
        value = ref[:, begin:begin + width]
        if width < LANES:
            value = jnp.concatenate([value, jnp.zeros((ROWS, LANES - width), F32)], axis=1)
        return value

    for unit in range(plan.used):
        c, p, k = plan.where(unit)
        for d in range(n_dp):
            g_ref[c, p, d, k] = jnp.concatenate(
                [half_unit(2 * unit, d), half_unit(2 * unit + 1, d)], axis=0
            ).astype(BF16)

    core_copy = pltpu.make_async_remote_copy(
        src_ref=g_ref.at[1 - core], dst_ref=r1_ref, send_sem=core_send, recv_sem=core_recv,
        device_id=partner, device_id_type=MESH,
    )
    core_copy.start()
    pending = []

    def plane_stage():
        core_copy.wait_recv()
        s1_ref[...] = (g_ref[core].astype(F32) + r1_ref[...].astype(F32)).astype(BF16)
        for j in range(1, n_plane):
            other = lax.rem(mine + j, n_plane)
            copy = pltpu.make_async_remote_copy(
                src_ref=s1_ref.at[other], dst_ref=r2_ref.at[j],
                send_sem=plane_send.at[j], recv_sem=plane_recv.at[j],
                device_id=in_plane(other, core), device_id_type=MESH,
            )
            copy.start()
            pending.append(copy)

    def dp_stage():
        total = s1_ref[mine].astype(F32)
        for j in range(1, n_plane):
            pending[j - 1].wait_recv()
            total = total + r2_ref[j].astype(F32)
        s2_ref[...] = total.astype(BF16)
        for j in range(1, n_dp):
            other = lax.rem(dp + j, n_dp)
            copy = pltpu.make_async_remote_copy(
                src_ref=s2_ref.at[other], dst_ref=r3_ref.at[j],
                send_sem=dp_send.at[j], recv_sem=dp_recv.at[j],
                device_id={"grp": grp, "dp": other, "seq": seq}, device_id_type=MESH,
            )
            copy.start()
            pending.append(copy)

    def gather_stage():
        total = s2_ref[dp].astype(F32)
        for j in range(1, n_dp):
            pending[n_plane - 1 + j - 1].wait_recv()
            total = total + r3_ref[j].astype(F32)
        a_ref[core, mine] = total.astype(BF16)
        for j in range(n_plane):
            for flip in range(2):
                if j == 0 and flip == 0:
                    continue
                copy = pltpu.make_async_remote_copy(
                    src_ref=a_ref.at[core, mine], dst_ref=a_ref.at[core, mine],
                    send_sem=all_send.at[2 * j + flip], recv_sem=all_recv.at[2 * j + flip],
                    device_id=in_plane(lax.rem(mine + j, n_plane), core + flip * (1 - 2 * core)),
                    device_id_type=MESH,
                )
                copy.start()
                pending.append(copy)

    for copy in kv_copies:
        copy.wait_recv()
    loads[9].wait()
    queries = tq_ref.shape[0]
    keys = k_ref.shape[1]
    own_pos = pos_ref[0].astype(F32)
    for begin in range(0, queries, LANES):
        column = jnp.transpose(jnp.broadcast_to(own_pos[:, begin:begin + LANES], (LANES, LANES)))
        for j in range(n_seq):
            key_pos = pos_ref[j].astype(F32)
            for at in range(0, keys, LANES):
                bias_ref[begin:begin + LANES, j * keys + at:j * keys + at + LANES] = jnp.where(
                    key_pos[:, at:at + LANES] <= column, 0.0, MASKED
                )
    heads = tq_ref.shape[1] // HEAD_SIZE
    group = heads // (k_ref.shape[2] // HEAD_SIZE)
    factor = HEAD_SIZE ** (-0.5) * LOG2E
    stages = {1 * heads // 14: plane_stage, 7 * heads // 14: dp_stage, 12 * heads // 14: gather_stage}
    ones_v = jnp.ones((n_seq * keys, HEAD_SIZE), BF16)
    for h in range(heads):
        if h in stages:
            stages[h]()
        at = h // group * HEAD_SIZE
        k_all = k_ref[:, :, at:at + HEAD_SIZE].reshape(n_seq * keys, HEAD_SIZE)
        v_all = jnp.concatenate(
            [v_ref[:, :, at:at + HEAD_SIZE].reshape(n_seq * keys, HEAD_SIZE), ones_v], axis=1
        )
        score = dot(tq_ref[:, h * HEAD_SIZE:(h + 1) * HEAD_SIZE], k_all, ((1,), (1,))) + bias_ref[...]
        top = jnp.max(score, axis=1, keepdims=True)
        weight = jnp.exp2((score - top) * factor).astype(BF16)
        mixed = dot(weight, v_all)
        out_ref[0, :, h * HEAD_SIZE:(h + 1) * HEAD_SIZE] = (
            mixed[:, :HEAD_SIZE] / mixed[:, HEAD_SIZE:]
        ).astype(BF16)

    for copy in pending[n_plane - 1 + n_dp - 1:]:
        copy.wait_recv()
    for index, (which, row, begin, width) in enumerate(plan.halves):
        c, p, k = plan.where(index // 2)
        half = index % 2 * ROWS
        value = a_ref[c, p, k].astype(F32)[half:half + ROWS, :width]
        (gf_out, gd_out, gu_out)[which][row:row + ROWS, begin:begin + width] = value
    core_copy.wait_send()
    for copy in kv_copies + pending:
        copy.wait_send()


def on_device(mesh_shape, *args):
    x, sq, cot, w, ad, au, tq, tk, tv, pos = args
    n_grp, n_dp, n_seq = mesh_shape["grp"], mesh_shape["dp"], mesh_shape["seq"]
    plan = Plan(n_grp, n_dp, n_seq, w.shape, x.shape[2], sq.shape[2])
    n_plane, per = plan.plane, plan.per
    rows, queries, keys = sq.shape[1], tq.shape[1], tk.shape[1]
    vm, dma = pltpu.VMEM, pltpu.SemaphoreType.DMA
    unit = (16, LANES)
    return pl.pallas_call(
        functools.partial(kernel, plan),
        out_shape=(
            jax.ShapeDtypeStruct(tq.shape, BF16),
            jax.ShapeDtypeStruct((plan.feature_rows, w.shape[1]), F32),
            jax.ShapeDtypeStruct((ad.shape[0], plan.down_width), F32),
            jax.ShapeDtypeStruct((au.shape[0], plan.up_width), F32),
        ),
        in_specs=[pl.BlockSpec(memory_space=pl.ANY)] * 10,
        out_specs=[pl.BlockSpec(memory_space=pltpu.VMEM)] * 4,
        scratch_shapes=[
            vm(x.shape[1:], BF16), vm(sq.shape[1:], BF16), vm(cot.shape[1:], BF16), vm(w.shape, BF16),
            vm(ad.shape, BF16), vm(au.shape, BF16), vm(tq.shape[1:], BF16),
            vm((n_seq, keys, tk.shape[2]), BF16), vm((n_seq, keys, tv.shape[2]), BF16),
            vm((n_seq, 1, keys), jnp.int32),
            vm((queries, n_seq * keys), F32), vm((rows, sq.shape[2]), BF16),
            vm(w.shape, F32), vm(ad.shape, F32), vm(au.shape, F32),
            vm((2, n_plane, n_dp, per) + unit, BF16),
            vm((n_plane, n_dp, per) + unit, BF16), vm((n_plane, n_dp, per) + unit, BF16),
            vm((n_plane, n_dp, per) + unit, BF16),
            vm((n_dp, per) + unit, BF16), vm((n_dp, per) + unit, BF16),
            vm((2, n_plane, per) + unit, BF16),
            dma((10,)), dma((3, n_seq)), dma((3, n_seq)), dma, dma,
            dma((n_plane,)), dma((n_plane,)), dma((n_dp,)), dma((n_dp,)),
            dma((2 * n_plane,)), dma((2 * n_plane,)),
        ],
        compiler_params=pltpu.CompilerParams(
            collective_id=0, has_side_effects=True, vmem_limit_bytes=48 * 2**20
        ),
    )(*args)


def solution(mesh):
    rows = P(("grp", "dp"), "seq", None)
    return jax.shard_map(
        functools.partial(on_device, dict(mesh.shape)),
        mesh=mesh,
        in_specs=(rows, rows, rows, P(), P(), P(), rows, rows, rows, P(("grp", "dp"), "seq")),
        out_specs=(rows, P("dp", None), P(None, "dp"), P(None, "dp")),
        check_vma=False,
    )
```

time: 153 us -> 39.9 us (0.26)
  waiting for transfers between devices: 87.6 us -> 0 us
  Pallas kernels: 0 us -> 26.6 us
  blocking collectives: 16.5 us -> 0 us
  between operations: 14 us -> 0.66 us
  matrix products: 12.1 us -> 0 us
  other arithmetic: 6.57 us -> 0 us
  local copies, waits for them, and re-layouts: 16 us -> 12.2 us
    psum x2 -> x0, waiting for transfers between devices: 42.1 us -> none  [the longest x1 25.7 us: reduce_grads(): lax.psum(shards[0].astype(jnp.bfloat16), 'grp').astype(jnp.float32)]
    pallas_call x0 -> x1, Pallas kernels: none -> 26.6 us  [on_device(): pl.pallas_call(functools.partial(kernel, plan), out_shape=(jax.ShapeDtype...]
    unnamed x7 -> x0, waiting for transfers between devices: 26.1 us -> none
    reduce_scatter x1 -> x0, waiting for transfers between devices: 19.4 us -> none  [reduce_grads(): lax.psum_scatter(along_seq[0].astype(jnp.bfloat16), 'dp', scatter_dimensi...]
    all_gather x3 -> x0, blocking collectives: 16.5 us -> none  [the longest x1 5.65 us: teacher_attention(): key_piece = lax.all_gather(teacher_next_key, 'seq', axis=1, tiled=True)]
    dot_general x6 -> x0, matrix products: 10.7 us -> none  [the longest x1 5.15 us: one_block(): jnp.einsum('cgqk,kcd->qcgd', weights.astype(jnp.bfloat16), rows_of_values...]
    convert_element_type x3 -> x0, other arithmetic: 4.1 us -> none  [the longest x1 1.47 us: reduce_grads(): lax.psum(shards[0].astype(jnp.bfloat16), 'grp').astype(jnp.float32)]
    convert_element_type x2 -> x0, local copies, waits for them, and re-layouts: 2.06 us -> none  [the longest x1 1.22 us: student_gradients(): feature_cotangent.reshape(row_count, head_count, 2 * F).astype(jnp.float32)]
  transfers between devices with their start and end apart: 5 -> 0, of which waited for: 5 -> 0; matrix products, arithmetic and copies ran while one was open for 12% -> 0% of each run, Pallas kernels for 0% -> 0%
where the time goes in v1:
time: 39.9 us; the launch traced here: 39.4 us
  Pallas kernels  26.6 us (67%)
  local copies, waits for them, and re-layouts  12.2 us (31%)
  between operations  0.66 us (2%)
    pallas_call x1, Pallas kernels, on_device(): pl.pallas_call(functools.partial(kernel, plan), out_shape=(jax.ShapeDtype...  26.6 us
    unnamed x24, local copies, waits for them, and re-layouts  12.2 us

profile of v1, /device:TPU:0, one launch (start us, length us, event | category | flops | bytes accessed | tf_op | source)
XLA Modules:
  0.0 39.4 jit_solution(10616727544394444586)
XLA Ops:
  0.6 0.0 copy-start
  0.6 1.2 %copy-done = bf16[1,128,3584]{2,1,0:T(8,128)(2,1)S(1)} copy-done((bf16[1,128,3584]{2,1,0:T(8,128)(2,1)S(1)}, bf16[1,128,3584]{2,1,0:T(8,128)(2,1)}, u32[]{:S(2)}) %copy-start) | copy-done | bytes 917528
  1.8 0.0 copy-start.1
  1.8 1.2 %copy-done.1 = bf16[1,256,1792]{2,1,0:T(8,128)(2,1)S(1)} copy-done((bf16[1,256,1792]{2,1,0:T(8,128)(2,1)S(1)}, bf16[1,256,1792]{2,1,0:T(8,128)(2,1)}, u32[]{:S(2)}) %copy-start.1) | copy-done | bytes 917528
  3.0 0.0 copy-start.2
  3.0 1.0 %copy-done.2 = bf16[1,128,1792]{2,1,0:T(8,128)(2,1)S(1)} copy-done((bf16[1,128,1792]{2,1,0:T(8,128)(2,1)S(1)}, bf16[1,128,1792]{2,1,0:T(8,128)(2,1)}, u32[]{:S(2)}) %copy-start.2) | copy-done | bytes 458776
  4.0 0.0 copy-start.3
  4.0 1.0 %copy-done.3 = bf16[1,128,1792]{2,1,0:T(8,128)(2,1)S(1)} copy-done((bf16[1,128,1792]{2,1,0:T(8,128)(2,1)S(1)}, bf16[1,128,1792]{2,1,0:T(8,128)(2,1)}, u32[]{:S(2)}) %copy-start.3) | copy-done | bytes 458776
  5.0 0.0 copy-start.4
  5.0 0.9 %copy-done.4 = bf16[128,896]{1,0:T(8,128)(2,1)S(1)} copy-done((bf16[128,896]{1,0:T(8,128)(2,1)S(1)}, bf16[128,896]{1,0:T(8,128)(2,1)}, u32[]{:S(2)}) %copy-start.4) | copy-done | bytes 229400
  6.0 0.0 copy-start.5
  6.0 0.9 %copy-done.5 = bf16[1,256,256]{2,1,0:T(8,128)(2,1)S(1)} copy-done((bf16[1,256,256]{2,1,0:T(8,128)(2,1)S(1)}, bf16[1,256,256]{2,1,0:T(8,128)(2,1)}, u32[]{:S(2)}) %copy-start.5) | copy-done | bytes 131096
  6.9 0.0 copy-start.6
  6.9 0.9 %copy-done.6 = bf16[1,256,256]{2,1,0:T(8,128)(2,1)S(1)} copy-done((bf16[1,256,256]{2,1,0:T(8,128)(2,1)S(1)}, bf16[1,256,256]{2,1,0:T(8,128)(2,1)}, u32[]{:S(2)}) %copy-start.6) | copy-done | bytes 131096
  7.8 0.0 copy-start.7
  7.8 0.8 %copy-done.7 = bf16[8,3584]{1,0:T(8,128)(2,1)S(1)} copy-done((bf16[8,3584]{1,0:T(8,128)(2,1)S(1)}, bf16[8,3584]{1,0:T(8,128)(2,1)}, u32[]{:S(2)}) %copy-start.7) | copy-done | bytes 57368
  8.6 0.0 copy-start.8
  8.6 0.7 %copy-done.8 = bf16[8,1792]{1,0:T(8,128)(2,1)S(1)} copy-done((bf16[8,1792]{1,0:T(8,128)(2,1)S(1)}, bf16[8,1792]{1,0:T(8,128)(2,1)}, u32[]{:S(2)}) %copy-start.8) | copy-done | bytes 28696
  9.4 0.7 %copy-done.9 = s32[1,256]{1,0:T(1,128)S(1)} copy-done((s32[1,256]{1,0:T(1,128)S(1)}, s32[1,256]{1,0:T(1,128)}, u32[]{:S(2)}) %copy-start.9) | copy-done | bytes 1048
  10.0 26.6 %shard_map.129 = (bf16[1,256,1792]{2,1,0:T(8,128)(2,1)S(1)}, f32[32,896]{1,0:T(8,128)S(1)}, f32[8,896]{1,0:T(8,128)S(1)}, f32[8,448]{1,0:T(8,128)S(1)}) custom-call(bf16[1,128,3584]{2,1,0:T(8,128)(2,1)S(1)} %copy-done, bf16[1,128,1792]{2,1,0:T(8,128)(2,1)S(1)} %copy-done.2, bf16[1,128,1792]{2,1,0:T(8,128)(2,1)S(1)} %copy-done.3, ...), custom_call_target="tpu_custom_call" | custom-call | tf_op jit(solution)/shard_map/pallas_call | solution.py:295
  36.6 0.9 %copy.18 = bf16[1,256,1792]{2,1,0:T(8,128)(2,1)} copy(bf16[1,256,1792]{2,1,0:T(8,128)(2,1)S(1)} %get-tuple-element.8) | data formatting | bytes 1835008
  37.5 0.6 %copy.19 = f32[32,896]{1,0:T(8,128)} copy(f32[32,896]{1,0:T(8,128)S(1)} %get-tuple-element.9) | data formatting | bytes 229376
  38.2 0.6 %copy.20 = f32[8,896]{1,0:T(8,128)} copy(f32[8,896]{1,0:T(8,128)S(1)} %get-tuple-element.10) | data formatting | bytes 57344
  38.8 0.6 %copy.21 = f32[8,448]{1,0:T(8,128)} copy(f32[8,448]{1,0:T(8,128)S(1)} %get-tuple-element.11) | data formatting | bytes 28672
  (1 shorter events, 0.0 us)
Async XLA Ops:
  0.6 1.2 %copy-start = (bf16[1,128,3584]{2,1,0:T(8,128)(2,1)S(1)}, bf16[1,128,3584]{2,1,0:T(8,128)(2,1)}, u32[]{:S(2)}) copy-start(bf16[1,128,3584]{2,1,0:T(8,128)(2,1)} %x_hbm.1) | copy-start | bytes 2752516
  1.8 1.2 %copy-start.1 = (bf16[1,256,1792]{2,1,0:T(8,128)(2,1)S(1)}, bf16[1,256,1792]{2,1,0:T(8,128)(2,1)}, u32[]{:S(2)}) copy-start(bf16[1,256,1792]{2,1,0:T(8,128)(2,1)} %tq_hbm.1) | copy-start | bytes 2752516
  3.0 1.0 %copy-start.2 = (bf16[1,128,1792]{2,1,0:T(8,128)(2,1)S(1)}, bf16[1,128,1792]{2,1,0:T(8,128)(2,1)}, u32[]{:S(2)}) copy-start(bf16[1,128,1792]{2,1,0:T(8,128)(2,1)} %sq_hbm.1) | copy-start | bytes 1376260
  4.0 1.0 %copy-start.3 = (bf16[1,128,1792]{2,1,0:T(8,128)(2,1)S(1)}, bf16[1,128,1792]{2,1,0:T(8,128)(2,1)}, u32[]{:S(2)}) copy-start(bf16[1,128,1792]{2,1,0:T(8,128)(2,1)} %cot_hbm.1) | copy-start | bytes 1376260
  5.0 0.9 %copy-start.4 = (bf16[128,896]{1,0:T(8,128)(2,1)S(1)}, bf16[128,896]{1,0:T(8,128)(2,1)}, u32[]{:S(2)}) copy-start(bf16[128,896]{1,0:T(8,128)(2,1)} %w_hbm.1) | copy-start | bytes 688132
  6.0 0.9 %copy-start.5 = (bf16[1,256,256]{2,1,0:T(8,128)(2,1)S(1)}, bf16[1,256,256]{2,1,0:T(8,128)(2,1)}, u32[]{:S(2)}) copy-start(bf16[1,256,256]{2,1,0:T(8,128)(2,1)} %tk_hbm.1) | copy-start | bytes 393220
  6.9 0.9 %copy-start.6 = (bf16[1,256,256]{2,1,0:T(8,128)(2,1)S(1)}, bf16[1,256,256]{2,1,0:T(8,128)(2,1)}, u32[]{:S(2)}) copy-start(bf16[1,256,256]{2,1,0:T(8,128)(2,1)} %tv_hbm.1) | copy-start | bytes 393220
  7.8 0.8 %copy-start.7 = (bf16[8,3584]{1,0:T(8,128)(2,1)S(1)}, bf16[8,3584]{1,0:T(8,128)(2,1)}, u32[]{:S(2)}) copy-start(bf16[8,3584]{1,0:T(8,128)(2,1)} %ad_hbm.1) | copy-start | bytes 172036
  8.6 0.7 %copy-start.8 = (bf16[8,1792]{1,0:T(8,128)(2,1)S(1)}, bf16[8,1792]{1,0:T(8,128)(2,1)}, u32[]{:S(2)}) copy-start(bf16[8,1792]{1,0:T(8,128)(2,1)} %au_hbm.1) | copy-start | bytes 86020
  9.3 0.7 %copy-start.9 = (s32[1,256]{1,0:T(1,128)S(1)}, s32[1,256]{1,0:T(1,128)}, u32[]{:S(2)}) copy-start(s32[1,256]{1,0:T(1,128)} %pos_hbm.1) | copy-start | bytes 3076

commit v2 on v1

--- a/solution.py
+++ b/solution.py
@@ -14,6 +14,8 @@
 ROWS = 8
 ADAPTER_SCALE = 2.0
 MASKED = -1e30
+VMEM_BYTES = 67043328
+PIECES = 4
 LOG2E = 1.4426950408889634
 BF16 = jnp.bfloat16
 F32 = jnp.float32
@@ -52,12 +54,12 @@
 def kernel(
     plan,
     x_hbm, sq_hbm, cot_hbm, w_hbm, ad_hbm, au_hbm, tq_hbm, tk_hbm, tv_hbm, pos_hbm,
-    out_ref, gf_out, gd_out, gu_out,
+    out_hbm, gf_out, gd_out, gu_out,
     x_ref, sq_ref, cot_ref, w_ref, ad_ref, au_ref, tq_ref, k_ref, v_ref, pos_ref,
     bias_ref, dq_ref, gf_ref, gd_ref, gu_ref,
     g_ref, r1_ref, s1_ref, r2_ref, s2_ref, r3_ref, a_ref,
     load_sem, kv_send, kv_recv, core_send, core_recv, plane_send, plane_recv,
-    dp_send, dp_recv, all_send, all_recv,
+    dp_send, dp_recv, all_send, all_recv, out_ref, out_sem,
 ):
     n_dp, n_seq, n_grp, n_plane, per = plan.n_dp, plan.n_seq, plan.n_grp, plan.plane, plan.per
     grp, dp, seq = lax.axis_index("grp"), lax.axis_index("dp"), lax.axis_index("seq")
@@ -256,6 +258,7 @@
     factor = HEAD_SIZE ** (-0.5) * LOG2E
     stages = {1 * heads // 14: plane_stage, 7 * heads // 14: dp_stage, 12 * heads // 14: gather_stage}
     ones_v = jnp.ones((n_seq * keys, HEAD_SIZE), BF16)
+    outs = []
     for h in range(heads):
         if h in stages:
             stages[h]()
@@ -268,9 +271,12 @@
         top = jnp.max(score, axis=1, keepdims=True)
         weight = jnp.exp2((score - top) * factor).astype(BF16)
         mixed = dot(weight, v_all)
-        out_ref[0, :, h * HEAD_SIZE:(h + 1) * HEAD_SIZE] = (
-            mixed[:, :HEAD_SIZE] / mixed[:, HEAD_SIZE:]
-        ).astype(BF16)
+        own = pl.ds(h * HEAD_SIZE, HEAD_SIZE)
+        out_ref[:, own] = (mixed[:, :HEAD_SIZE] / mixed[:, HEAD_SIZE:]).astype(BF16)
+        if h:
+            outs[-1].start()
+        outs.append(pltpu.make_async_copy(out_ref.at[:, own], out_hbm.at[0, :, own], out_sem.at[h]))
+    outs[-1].start()
 
     for copy in pending[n_plane - 1 + n_dp - 1:]:
         copy.wait_recv()
@@ -279,9 +285,33 @@
         half = index % 2 * ROWS
         value = a_ref[c, p, k].astype(F32)[half:half + ROWS, :width]
         (gf_out, gd_out, gu_out)[which][row:row + ROWS, begin:begin + width] = value
+    for copy in outs:
+        copy.wait()
     core_copy.wait_send()
     for copy in kv_copies + pending:
         copy.wait_send()
+
+
+def write_out(*refs):
+    sources, targets, held, load_sem, store_sem = refs[:4], refs[4:8], refs[8:12], refs[12], refs[13]
+    rows = sources[0].shape[1] // PIECES
+    parts = [(n, slice(None)) for n in range(1, 4)]
+    parts += [(0, (0, pl.ds(piece * rows, rows))) for piece in range(PIECES)]
+    loads = [
+        pltpu.make_async_copy(sources[n].at[at], held[n].at[at], load_sem.at[i])
+        for i, (n, at) in enumerate(parts)
+    ]
+    stores = [
+        pltpu.make_async_copy(held[n].at[at], targets[n].at[at], store_sem.at[i])
+        for i, (n, at) in enumerate(parts)
+    ]
+    for load in loads:
+        load.start()
+    for load, store in zip(loads, stores):
+        load.wait()
+        store.start()
+    for store in stores:
+        store.wait()
 
 
 def on_device(mesh_shape, *args):
@@ -292,16 +322,17 @@
     rows, queries, keys = sq.shape[1], tq.shape[1], tk.shape[1]
     vm, dma = pltpu.VMEM, pltpu.SemaphoreType.DMA
     unit = (16, LANES)
-    return pl.pallas_call(
+    shapes = (
+        jax.ShapeDtypeStruct(tq.shape, BF16),
+        jax.ShapeDtypeStruct((plan.feature_rows, w.shape[1]), F32),
+        jax.ShapeDtypeStruct((ad.shape[0], plan.down_width), F32),
+        jax.ShapeDtypeStruct((au.shape[0], plan.up_width), F32),
+    )
+    results = pl.pallas_call(
         functools.partial(kernel, plan),
-        out_shape=(
-            jax.ShapeDtypeStruct(tq.shape, BF16),
-            jax.ShapeDtypeStruct((plan.feature_rows, w.shape[1]), F32),
-            jax.ShapeDtypeStruct((ad.shape[0], plan.down_width), F32),
-            jax.ShapeDtypeStruct((au.shape[0], plan.up_width), F32),
-        ),
+        out_shape=shapes,
         in_specs=[pl.BlockSpec(memory_space=pl.ANY)] * 10,
-        out_specs=[pl.BlockSpec(memory_space=pltpu.VMEM)] * 4,
+        out_specs=[pl.BlockSpec(memory_space=pl.ANY)] + [pl.BlockSpec(memory_space=pltpu.VMEM)] * 3,
         scratch_shapes=[
             vm(x.shape[1:], BF16), vm(sq.shape[1:], BF16), vm(cot.shape[1:], BF16), vm(w.shape, BF16),
             vm(ad.shape, BF16), vm(au.shape, BF16), vm(tq.shape[1:], BF16),
@@ -317,11 +348,20 @@
             dma((10,)), dma((3, n_seq)), dma((3, n_seq)), dma, dma,
             dma((n_plane,)), dma((n_plane,)), dma((n_dp,)), dma((n_dp,)),
             dma((2 * n_plane,)), dma((2 * n_plane,)),
+            vm(tq.shape[1:], BF16), dma((tq.shape[2] // HEAD_SIZE,)),
         ],
         compiler_params=pltpu.CompilerParams(
-            collective_id=0, has_side_effects=True, vmem_limit_bytes=48 * 2**20
+            collective_id=0, has_side_effects=True, vmem_limit_bytes=VMEM_BYTES
         ),
     )(*args)
+    return pl.pallas_call(
+        write_out,
+        out_shape=shapes,
+        in_specs=[pl.BlockSpec(memory_space=pl.ANY)] * 4,
+        out_specs=[pl.BlockSpec(memory_space=pl.ANY)] * 4,
+        scratch_shapes=[vm(shape.shape, shape.dtype) for shape in shapes] + [dma((3 + PIECES,))] * 2,
+        compiler_params=pltpu.CompilerParams(vmem_limit_bytes=VMEM_BYTES),
+    )(*results)
 
 
 def solution(mesh):

time: 39.9 us -> 28.7 us (0.72)
  local copies, waits for them, and re-layouts: 12.2 us -> 0 us
  Pallas kernels: 26.6 us -> 27.8 us
    unnamed x24 -> x0, local copies, waits for them, and re-layouts: 12.2 us -> none
    pallas_call x1 -> x2, Pallas kernels: 26.6 us -> 27.8 us  [the longest x1 25.7 us: on_device(): pl.pallas_call(functools.partial(kernel, plan), out_shape=shapes, in_spec...]
where the time goes in v2:
time: 28.7 us; the launch traced here: 28.5 us
  Pallas kernels  27.8 us (97%)
  between operations  0.64 us (2%)
    pallas_call x1, Pallas kernels, on_device(): pl.pallas_call(functools.partial(kernel, plan), out_shape=shapes, in_spec...  25.7 us
    pallas_call x1, Pallas kernels, on_device(): pl.pallas_call(write_out, out_shape=shapes, in_specs=[pl.BlockSpec(memory...  2.14 us

profile of v2, /device:TPU:0, one launch (start us, length us, event | category | flops | bytes accessed | tf_op | source)
XLA Modules:
  0.0 28.5 jit_solution(434270011927588630)
XLA Ops:
  0.6 25.7 %shard_map.129 = (bf16[1,256,1792]{2,1,0:T(8,128)(2,1)}, f32[32,896]{1,0:T(8,128)}, f32[8,896]{1,0:T(8,128)}, f32[8,448]{1,0:T(8,128)}) custom-call(bf16[1,128,3584]{2,1,0:T(8,128)(2,1)} %x_hbm.1, bf16[1,128,1792]{2,1,0:T(8,128)(2,1)} %sq_hbm.1, bf16[1,128,1792]{2,1,0:T(8,128)(2,1)} %cot_hbm.1, bf16[128,896]{1,0:T(8,128)(2,1)} %w_hbm.1, ...), custom_call_target="tpu_custom_call" | custom-call | tf_op jit(solution)/shard_map/pallas_call | solution.py:331
  26.3 2.1 %shard_map.130 = (bf16[1,256,1792]{2,1,0:T(8,128)(2,1)}, f32[32,896]{1,0:T(8,128)}, f32[8,896]{1,0:T(8,128)}, f32[8,448]{1,0:T(8,128)}) custom-call(bf16[1,256,1792]{2,1,0:T(8,128)(2,1)} %get-tuple-element.8.refs_0_, f32[32,896]{1,0:T(8,128)} %get-tuple-element.9.refs_1_, f32[8,896]{1,0:T(8,128)} %get-tuple-element.10.refs_2_, ...), custom_call_target="tpu_custom_call" | custom-call | tf_op jit(solution)/shard_map/pallas_call | solution.py:357

commit v3 on v2

--- a/solution.py
+++ b/solution.py
@@ -16,6 +16,9 @@
 MASKED = -1e30
 VMEM_BYTES = 67043328
 PIECES = 4
+EARLY_PAIRS = 2
+EARLY_HEADS = 4
+STAGES = (1, 5, 12)
 LOG2E = 1.4426950408889634
 BF16 = jnp.bfloat16
 F32 = jnp.float32
@@ -54,12 +57,12 @@
 def kernel(
     plan,
     x_hbm, sq_hbm, cot_hbm, w_hbm, ad_hbm, au_hbm, tq_hbm, tk_hbm, tv_hbm, pos_hbm,
-    out_hbm, gf_out, gd_out, gu_out,
+    out_hbm, all_hbm,
     x_ref, sq_ref, cot_ref, w_ref, ad_ref, au_ref, tq_ref, k_ref, v_ref, pos_ref,
     bias_ref, dq_ref, gf_ref, gd_ref, gu_ref,
-    g_ref, r1_ref, s1_ref, r2_ref, s2_ref, r3_ref, a_ref,
+    g_ref, r1_ref, s1_ref, r2_ref, s2_ref, r3_ref, s3_ref, p_ref,
     load_sem, kv_send, kv_recv, core_send, core_recv, plane_send, plane_recv,
-    dp_send, dp_recv, all_send, all_recv, out_ref, out_sem,
+    dp_send, dp_recv, all_send, all_recv, out_ref, out_sem, own_sem,
 ):
     n_dp, n_seq, n_grp, n_plane, per = plan.n_dp, plan.n_seq, plan.n_grp, plan.plane, plan.per
     grp, dp, seq = lax.axis_index("grp"), lax.axis_index("dp"), lax.axis_index("seq")
@@ -101,21 +104,6 @@
         c, p, k = plan.where(unit)
         g_ref[c, p, :, k] = jnp.zeros((n_dp, 16, LANES), BF16)
 
-    for n in range(3):
-        loads[n].wait()
-    pl.semaphore_wait(barrier, greeted)
-
-    kv_copies = []
-    for n, ref in enumerate((pos_ref, k_ref, v_ref)):
-        for j in range(1, n_seq):
-            copy = pltpu.make_async_remote_copy(
-                src_ref=ref.at[0], dst_ref=ref.at[j],
-                send_sem=kv_send.at[n, j], recv_sem=kv_recv.at[n, j],
-                device_id={"grp": grp, "dp": dp, "seq": lax.rem(seq + j, n_seq)}, device_id_type=MESH,
-            )
-            copy.start()
-            kv_copies.append(copy)
-
     rows = sq_ref.shape[0]
     lane = lax.broadcasted_iota(jnp.int32, (rows, LANES), 1)
     first = lane < F
@@ -136,9 +124,28 @@
         sums = dot(jnp.concatenate([high, low], axis=1), ones)
         return [sums[n * rows:(n + 1) * rows] for n in range(len(values))]
 
+    kv_copies = []
+
+    def send_keys():
+        for n in range(3):
+            loads[n].wait()
+        pl.semaphore_wait(barrier, greeted)
+
+        for n, ref in enumerate((pos_ref, k_ref, v_ref)):
+            for j in range(1, n_seq):
+                copy = pltpu.make_async_remote_copy(
+                    src_ref=ref.at[0], dst_ref=ref.at[j],
+                    send_sem=kv_send.at[n, j], recv_sem=kv_recv.at[n, j],
+                    device_id={"grp": grp, "dp": dp, "seq": lax.rem(seq + j, n_seq)}, device_id_type=MESH,
+                )
+                copy.start()
+                kv_copies.append(copy)
+
     for n in range(3, 6):
         loads[n].wait()
     for j in range(w_ref.shape[1] // LANES):
+        if j == EARLY_PAIRS:
+            send_keys()
         q2 = sq_ref[:, 2 * LANES * j:2 * LANES * (j + 1)]
         w = w_ref[:, LANES * j:LANES * (j + 1)].astype(F32)
         w2 = jnp.concatenate([jnp.where(w_half, w, 0.0), jnp.where(w_half, 0.0, w)], axis=0).astype(BF16)
@@ -158,10 +165,12 @@
         dq_ref[:, 2 * LANES * j:2 * LANES * (j + 1)] = dot(dlogit_b, w2, ((1,), (1,))).astype(BF16)
     for n in range(6, 9):
         loads[n].wait()
-    down_act = dot(ad_ref[...], x_ref[...], ((1,), (1,))).astype(BF16)
-    gu_ref[...] = ADAPTER_SCALE * dot(down_act, dq_ref[...])
-    dlow = (ADAPTER_SCALE * dot(au_ref[...], dq_ref[...], ((1,), (1,)))).astype(BF16)
-    gd_ref[...] = dot(dlow, x_ref[...])
+    x = x_ref[...]
+    dq = dq_ref[...]
+    down_act = dot(x, ad_ref[...], ((1,), (1,))).astype(BF16)
+    dlow = (ADAPTER_SCALE * dot(dq, au_ref[...], ((1,), (1,)))).astype(BF16)
+    gu_ref[...] = ADAPTER_SCALE * dot(down_act, dq, ((0,), (0,)))
+    gd_ref[...] = dot(dlow, x, ((0,), (0,)))
 
     def half_unit(index, d):
         if index >= len(plan.halves):
@@ -190,6 +199,7 @@
     )
     core_copy.start()
     pending = []
+    own_piece = pltpu.make_async_copy(s3_ref, all_hbm.at[core, mine], own_sem)
 
     def plane_stage():
         core_copy.wait_recv()
@@ -225,13 +235,14 @@
         for j in range(1, n_dp):
             pending[n_plane - 1 + j - 1].wait_recv()
             total = total + r3_ref[j].astype(F32)
-        a_ref[core, mine] = total.astype(BF16)
+        s3_ref[...] = total.astype(BF16)
+        own_piece.start()
         for j in range(n_plane):
             for flip in range(2):
                 if j == 0 and flip == 0:
                     continue
                 copy = pltpu.make_async_remote_copy(
-                    src_ref=a_ref.at[core, mine], dst_ref=a_ref.at[core, mine],
+                    src_ref=s3_ref, dst_ref=all_hbm.at[core, mine],
                     send_sem=all_send.at[2 * j + flip], recv_sem=all_recv.at[2 * j + flip],
                     device_id=in_plane(lax.rem(mine + j, n_plane), core + flip * (1 - 2 * core)),
                     device_id_type=MESH,
@@ -239,7 +250,7 @@
                 copy.start()
                 pending.append(copy)
 
-    for copy in kv_copies:
+    for copy in kv_copies[:2 * (n_seq - 1)]:
         copy.wait_recv()
     loads[9].wait()
     queries = tq_ref.shape[0]
@@ -256,35 +267,46 @@
     heads = tq_ref.shape[1] // HEAD_SIZE
     group = heads // (k_ref.shape[2] // HEAD_SIZE)
     factor = HEAD_SIZE ** (-0.5) * LOG2E
-    stages = {1 * heads // 14: plane_stage, 7 * heads // 14: dp_stage, 12 * heads // 14: gather_stage}
+    stages = dict(zip(STAGES, (plane_stage, dp_stage, gather_stage)))
     ones_v = jnp.ones((n_seq * keys, HEAD_SIZE), BF16)
     outs = []
+
+    def weights(h):
+        at = h // group * HEAD_SIZE
+        k_all = k_ref[:, :, at:at + HEAD_SIZE].reshape(n_seq * keys, HEAD_SIZE)
+        score = dot(tq_ref[:, h * HEAD_SIZE:(h + 1) * HEAD_SIZE], k_all, ((1,), (1,))) + bias_ref[...]
+        top = jnp.max(score, axis=1, keepdims=True)
+        return jnp.exp2((score - top) * factor).astype(BF16)
+
+    def mix(h, weight):
+        at = h // group * HEAD_SIZE
+        v_all = jnp.concatenate(
+            [v_ref[:, :, at:at + HEAD_SIZE].reshape(n_seq * keys, HEAD_SIZE), ones_v], axis=1
+        )
+        mixed = dot(weight, v_all)
+        own = pl.ds(h * HEAD_SIZE, HEAD_SIZE)
+        out_ref[:, own] = (mixed[:, :HEAD_SIZE] / mixed[:, HEAD_SIZE:]).astype(BF16)
+        if outs:
+            outs[-1].start()
+        outs.append(pltpu.make_async_copy(out_ref.at[:, own], out_hbm.at[0, :, own], out_sem.at[h]))
+
     for h in range(heads):
         if h in stages:
             stages[h]()
-        at = h // group * HEAD_SIZE
-        k_all = k_ref[:, :, at:at + HEAD_SIZE].reshape(n_seq * keys, HEAD_SIZE)
-        v_all = jnp.concatenate(
-            [v_ref[:, :, at:at + HEAD_SIZE].reshape(n_seq * keys, HEAD_SIZE), ones_v], axis=1
-        )
-        score = dot(tq_ref[:, h * HEAD_SIZE:(h + 1) * HEAD_SIZE], k_all, ((1,), (1,))) + bias_ref[...]
-        top = jnp.max(score, axis=1, keepdims=True)
-        weight = jnp.exp2((score - top) * factor).astype(BF16)
-        mixed = dot(weight, v_all)
-        own = pl.ds(h * HEAD_SIZE, HEAD_SIZE)
-        out_ref[:, own] = (mixed[:, :HEAD_SIZE] / mixed[:, HEAD_SIZE:]).astype(BF16)
-        if h:
-            outs[-1].start()
-        outs.append(pltpu.make_async_copy(out_ref.at[:, own], out_hbm.at[0, :, own], out_sem.at[h]))
+        if h < EARLY_HEADS:
+            p_ref[h] = weights(h)
+        else:
+            if h == EARLY_HEADS:
+                for copy in kv_copies[2 * (n_seq - 1):]:
+                    copy.wait_recv()
+                for early in range(EARLY_HEADS):
+                    mix(early, p_ref[early])
+            mix(h, weights(h))
     outs[-1].start()
 
     for copy in pending[n_plane - 1 + n_dp - 1:]:
         copy.wait_recv()
-    for index, (which, row, begin, width) in enumerate(plan.halves):
-        c, p, k = plan.where(index // 2)
-        half = index % 2 * ROWS
-        value = a_ref[c, p, k].astype(F32)[half:half + ROWS, :width]
-        (gf_out, gd_out, gu_out)[which][row:row + ROWS, begin:begin + width] = value
+    own_piece.wait()
     for copy in outs:
         copy.wait()
     core_copy.wait_send()
@@ -292,24 +314,31 @@
         copy.wait_send()
 
 
-def write_out(*refs):
-    sources, targets, held, load_sem, store_sem = refs[:4], refs[4:8], refs[8:12], refs[12], refs[13]
-    rows = sources[0].shape[1] // PIECES
-    parts = [(n, slice(None)) for n in range(1, 4)]
-    parts += [(0, (0, pl.ds(piece * rows, rows))) for piece in range(PIECES)]
+def write_out(plan, out_hbm, all_hbm, out, gf_out, gd_out, gu_out,
+              out_vm, all_vm, gf_vm, gd_vm, gu_vm, load_sem, store_sem):
+    rows = out_vm.shape[1] // PIECES
+    parts = [(0, pl.ds(piece * rows, rows)) for piece in range(PIECES)]
+    gathered = pltpu.make_async_copy(all_hbm, all_vm, load_sem.at[PIECES])
+    gathered.start()
     loads = [
-        pltpu.make_async_copy(sources[n].at[at], held[n].at[at], load_sem.at[i])
-        for i, (n, at) in enumerate(parts)
+        pltpu.make_async_copy(out_hbm.at[at], out_vm.at[at], load_sem.at[i]) for i, at in enumerate(parts)
     ]
     stores = [
-        pltpu.make_async_copy(held[n].at[at], targets[n].at[at], store_sem.at[i])
-        for i, (n, at) in enumerate(parts)
+        pltpu.make_async_copy(out_vm.at[at], out.at[at], store_sem.at[i]) for i, at in enumerate(parts)
     ]
     for load in loads:
         load.start()
+    gathered.wait()
+    for index, (which, row, begin, width) in enumerate(plan.halves):
+        half = index % 2 * ROWS
+        value = all_vm[plan.where(index // 2)].astype(F32)[half:half + ROWS, :width]
+        (gf_vm, gd_vm, gu_vm)[which][row:row + ROWS, begin:begin + width] = value
     for load, store in zip(loads, stores):
         load.wait()
         store.start()
+    for n, (held, target) in enumerate(((gf_vm, gf_out), (gd_vm, gd_out), (gu_vm, gu_out))):
+        stores.append(pltpu.make_async_copy(held, target, store_sem.at[PIECES + n]))
+        stores[-1].start()
     for store in stores:
         store.wait()
 
@@ -330,9 +359,9 @@
     )
     results = pl.pallas_call(
         functools.partial(kernel, plan),
-        out_shape=shapes,
+        out_shape=(shapes[0], jax.ShapeDtypeStruct((2, n_plane, per) + unit, BF16)),
         in_specs=[pl.BlockSpec(memory_space=pl.ANY)] * 10,
-        out_specs=[pl.BlockSpec(memory_space=pl.ANY)] + [pl.BlockSpec(memory_space=pltpu.VMEM)] * 3,
+        out_specs=[pl.BlockSpec(memory_space=pl.ANY)] * 2,
         scratch_shapes=[
             vm(x.shape[1:], BF16), vm(sq.shape[1:], BF16), vm(cot.shape[1:], BF16), vm(w.shape, BF16),
             vm(ad.shape, BF16), vm(au.shape, BF16), vm(tq.shape[1:], BF16),
@@ -344,22 +373,23 @@
             vm((n_plane, n_dp, per) + unit, BF16), vm((n_plane, n_dp, per) + unit, BF16),
             vm((n_plane, n_dp, per) + unit, BF16),
             vm((n_dp, per) + unit, BF16), vm((n_dp, per) + unit, BF16),
-            vm((2, n_plane, per) + unit, BF16),
+            vm((per,) + unit, BF16), vm((EARLY_HEADS, queries, n_seq * keys), BF16),
             dma((10,)), dma((3, n_seq)), dma((3, n_seq)), dma, dma,
             dma((n_plane,)), dma((n_plane,)), dma((n_dp,)), dma((n_dp,)),
             dma((2 * n_plane,)), dma((2 * n_plane,)),
-            vm(tq.shape[1:], BF16), dma((tq.shape[2] // HEAD_SIZE,)),
+            vm(tq.shape[1:], BF16), dma((tq.shape[2] // HEAD_SIZE,)), dma,
         ],
         compiler_params=pltpu.CompilerParams(
             collective_id=0, has_side_effects=True, vmem_limit_bytes=VMEM_BYTES
         ),
     )(*args)
     return pl.pallas_call(
-        write_out,
+        functools.partial(write_out, plan),
         out_shape=shapes,
-        in_specs=[pl.BlockSpec(memory_space=pl.ANY)] * 4,
+        in_specs=[pl.BlockSpec(memory_space=pl.ANY)] * 2,
         out_specs=[pl.BlockSpec(memory_space=pl.ANY)] * 4,
-        scratch_shapes=[vm(shape.shape, shape.dtype) for shape in shapes] + [dma((3 + PIECES,))] * 2,
+        scratch_shapes=[vm(tq.shape, BF16), vm((2, n_plane, per) + unit, BF16)]
+        + [vm(shape.shape, F32) for shape in shapes[1:]] + [dma((3 + PIECES,))] * 2,
         compiler_params=pltpu.CompilerParams(vmem_limit_bytes=VMEM_BYTES),
     )(*results)
 

time: 28.7 us -> 26.9 us (0.937)
  Pallas kernels: 27.8 us -> 26.1 us
    pallas_call x2, Pallas kernels: 27.8 us -> 26.1 us  [the longest x1 24 us: on_device(): pl.pallas_call(functools.partial(kernel, plan), out_shape=(shapes[0], jax...]
where the time goes in v3:
time: 26.9 us; the launch traced here: 26.8 us
  Pallas kernels  26.1 us (97%)
  between operations  0.64 us (2%)
    pallas_call x1, Pallas kernels, on_device(): pl.pallas_call(functools.partial(kernel, plan), out_shape=(shapes[0], jax...  24 us
    pallas_call x1, Pallas kernels, on_device(): pl.pallas_call(functools.partial(write_out, plan), out_shape=shapes, in_s...  2.14 us

profile of v3, /device:TPU:0, one launch (start us, length us, event | category | flops | bytes accessed | tf_op | source)
XLA Modules:
  0.0 26.8 jit_solution(14481175962118802481)
XLA Ops:
  0.6 24.0 %shard_map.129 = (bf16[1,256,1792]{2,1,0:T(8,128)(2,1)}, bf16[2,4,3,16,128]{4,3,2,1,0:T(8,128)(2,1)}) custom-call(bf16[1,128,3584]{2,1,0:T(8,128)(2,1)} %x_hbm.1, bf16[1,128,1792]{2,1,0:T(8,128)(2,1)} %sq_hbm.1, bf16[1,128,1792]{2,1,0:T(8,128)(2,1)} %cot_hbm.1, bf16[128,896]{1,0:T(8,128)(2,1)} %w_hbm.1, bf16[8,3584]{1,0:T(8,128)(2,1)} %ad_hbm.1, ...), custom_call_target="tpu_custom_call" | custom-call | tf_op jit(solution)/shard_map/pallas_call | solution.py:360
  24.6 2.1 %shard_map.130 = (bf16[1,256,1792]{2,1,0:T(8,128)(2,1)}, f32[32,896]{1,0:T(8,128)}, f32[8,896]{1,0:T(8,128)}, f32[8,448]{1,0:T(8,128)}) custom-call(bf16[1,256,1792]{2,1,0:T(8,128)(2,1)} %get-tuple-element.6.out_hbm, bf16[2,4,3,16,128]{4,3,2,1,0:T(8,128)(2,1)} %get-tuple-element.7.all_hbm), custom_call_target="tpu_custom_call" | custom-call | tf_op jit(solution)/shard_map/pallas_call | solution.py:386

commit v4 on v3

--- a/solution.py
+++ b/solution.py
@@ -17,8 +17,8 @@
 VMEM_BYTES = 67043328
 PIECES = 4
 EARLY_PAIRS = 2
-EARLY_HEADS = 4
-STAGES = (1, 5, 12)
+PAIR_GROUP = 3
+STAGES = (1, 13, 22)
 LOG2E = 1.4426950408889634
 BF16 = jnp.bfloat16
 F32 = jnp.float32
@@ -75,9 +75,9 @@
     loads = []
     for n, (src, dst) in enumerate(
         (
-            (pos_hbm, pos_ref.at[0]), (tk_hbm.at[0], k_ref.at[0]), (tv_hbm.at[0], v_ref.at[0]),
-            (w_hbm, w_ref), (sq_hbm.at[0], sq_ref), (cot_hbm.at[0], cot_ref), (ad_hbm, ad_ref),
-            (x_hbm.at[0], x_ref), (au_hbm, au_ref), (tq_hbm.at[0], tq_ref),
+            (w_hbm, w_ref), (sq_hbm.at[0], sq_ref), (cot_hbm.at[0], cot_ref),
+            (pos_hbm, pos_ref.at[0]), (tk_hbm.at[0], k_ref.at[0]), (ad_hbm, ad_ref),
+            (x_hbm.at[0], x_ref), (au_hbm, au_ref), (tv_hbm.at[0], v_ref.at[0]), (tq_hbm.at[0], tq_ref),
         )
     ):
         copy = pltpu.make_async_copy(src, dst, load_sem.at[n])
@@ -126,12 +126,8 @@
 
     kv_copies = []
 
-    def send_keys():
-        for n in range(3):
-            loads[n].wait()
-        pl.semaphore_wait(barrier, greeted)
-
-        for n, ref in enumerate((pos_ref, k_ref, v_ref)):
+    def send(first_array, *refs):
+        for n, ref in enumerate(refs, first_array):
             for j in range(1, n_seq):
                 copy = pltpu.make_async_remote_copy(
                     src_ref=ref.at[0], dst_ref=ref.at[j],
@@ -141,29 +137,49 @@
                 copy.start()
                 kv_copies.append(copy)
 
-    for n in range(3, 6):
+    for n in range(3):
         loads[n].wait()
-    for j in range(w_ref.shape[1] // LANES):
-        if j == EARLY_PAIRS:
-            send_keys()
+    def begin_pair(j):
         q2 = sq_ref[:, 2 * LANES * j:2 * LANES * (j + 1)]
         w = w_ref[:, LANES * j:LANES * (j + 1)].astype(F32)
         w2 = jnp.concatenate([jnp.where(w_half, w, 0.0), jnp.where(w_half, 0.0, w)], axis=0).astype(BF16)
         logit = dot(q2, w2)
+        return q2, w2, logit
+
+    def mid_pair(j, q2, w2, logit):
         plus = jnp.exp(logit - half_max(logit))
         minus = jnp.exp(-logit - half_max(-logit))
         cot_a = cot_ref[:, 2 * LANES * j:2 * LANES * j + LANES].astype(F32)
         cot_b = cot_ref[:, 2 * LANES * j + LANES:2 * LANES * (j + 1)].astype(F32)
         cot_plus = jnp.where(first, cot_a, pltpu.roll(cot_b, F, 1))
         cot_minus = jnp.where(first, pltpu.roll(cot_a, F, 1), cot_b)
-        sum_p, sum_m, sum_pc, sum_mc = half_sum([plus, minus, plus * cot_plus, minus * cot_minus])
+        sums = half_sum([plus, minus, plus * cot_plus, minus * cot_minus])
+        return q2, w2, plus, minus, cot_plus, cot_minus, sums
+
+    def end_pair(j, q2, w2, plus, minus, cot_plus, cot_minus, sums):
+        sum_p, sum_m, sum_pc, sum_mc = sums
         inv_p, inv_m = 1.0 / sum_p, 1.0 / sum_m
         dlogit = plus * inv_p * (cot_plus - sum_pc * inv_p) - minus * inv_m * (cot_minus - sum_mc * inv_m)
         dlogit_b = dlogit.astype(BF16)
         grad = dot(q2, dlogit_b, ((0,), (0,)))
         gf_ref[:, LANES * j:LANES * (j + 1)] = jnp.where(w_half, grad[:HEAD_SIZE], grad[HEAD_SIZE:])
         dq_ref[:, 2 * LANES * j:2 * LANES * (j + 1)] = dot(dlogit_b, w2, ((1,), (1,))).astype(BF16)
-    for n in range(6, 9):
+
+    def student_pairs(begin, end):
+        states = [begin_pair(j) for j in range(begin, end)]
+        states = [mid_pair(j, *state) for j, state in zip(range(begin, end), states)]
+        for j, state in zip(range(begin, end), states):
+            end_pair(j, *state)
+
+    pairs = w_ref.shape[1] // LANES
+    student_pairs(0, EARLY_PAIRS)
+    for n in range(3, 5):
+        loads[n].wait()
+    pl.semaphore_wait(barrier, greeted)
+    send(0, pos_ref, k_ref)
+    for begin in range(EARLY_PAIRS, pairs, PAIR_GROUP):
+        student_pairs(begin, min(begin + PAIR_GROUP, pairs))
+    for n in range(5, 8):
         loads[n].wait()
     x = x_ref[...]
     dq = dq_ref[...]
@@ -213,6 +229,8 @@
             )
             copy.start()
             pending.append(copy)
+        loads[8].wait()
+        send(2, v_ref)
 
     def dp_stage():
         total = s1_ref[mine].astype(F32)
@@ -290,18 +308,16 @@
             outs[-1].start()
         outs.append(pltpu.make_async_copy(out_ref.at[:, own], out_hbm.at[0, :, own], out_sem.at[h]))
 
-    for h in range(heads):
-        if h in stages:
-            stages[h]()
-        if h < EARLY_HEADS:
-            p_ref[h] = weights(h)
+    for step in range(2 * heads):
+        if step in stages:
+            stages[step]()
+        if step == heads:
+            for copy in kv_copies[2 * (n_seq - 1):]:
+                copy.wait_recv()
+        if step < heads:
+            p_ref[step] = weights(step)
         else:
-            if h == EARLY_HEADS:
-                for copy in kv_copies[2 * (n_seq - 1):]:
-                    copy.wait_recv()
-                for early in range(EARLY_HEADS):
-                    mix(early, p_ref[early])
-            mix(h, weights(h))
+            mix(step - heads, p_ref[step - heads])
     outs[-1].start()
 
     for copy in pending[n_plane - 1 + n_dp - 1:]:
@@ -373,7 +389,7 @@
             vm((n_plane, n_dp, per) + unit, BF16), vm((n_plane, n_dp, per) + unit, BF16),
             vm((n_plane, n_dp, per) + unit, BF16),
             vm((n_dp, per) + unit, BF16), vm((n_dp, per) + unit, BF16),
-            vm((per,) + unit, BF16), vm((EARLY_HEADS, queries, n_seq * keys), BF16),
+            vm((per,) + unit, BF16), vm((tq.shape[2] // HEAD_SIZE, queries, n_seq * keys), BF16),
             dma((10,)), dma((3, n_seq)), dma((3, n_seq)), dma, dma,
             dma((n_plane,)), dma((n_plane,)), dma((n_dp,)), dma((n_dp,)),
             dma((2 * n_plane,)), dma((2 * n_plane,)),

time: 26.9 us -> 25.8 us (0.959)
  Pallas kernels: 26.1 us -> 25 us
    pallas_call x1, Pallas kernels: 24 us -> 22.8 us  [on_device(): pl.pallas_call(functools.partial(kernel, plan), out_shape=(shapes[0], jax...]
where the time goes in v4:
time: 25.8 us; the launch traced here: 25.6 us
  Pallas kernels  25 us (97%)
  between operations  0.64 us (2%)
    pallas_call x1, Pallas kernels, on_device(): pl.pallas_call(functools.partial(kernel, plan), out_shape=(shapes[0], jax...  22.8 us
    pallas_call x1, Pallas kernels, on_device(): pl.pallas_call(functools.partial(write_out, plan), out_shape=shapes, in_s...  2.14 us

profile of v4, /device:TPU:0, one launch (start us, length us, event | category | flops | bytes accessed | tf_op | source)
XLA Modules:
  0.0 25.6 jit_solution(6540754994021469655)
XLA Ops:
  0.6 22.8 %shard_map.129 = (bf16[1,256,1792]{2,1,0:T(8,128)(2,1)}, bf16[2,4,3,16,128]{4,3,2,1,0:T(8,128)(2,1)}) custom-call(bf16[1,128,3584]{2,1,0:T(8,128)(2,1)} %x_hbm.1, bf16[1,128,1792]{2,1,0:T(8,128)(2,1)} %sq_hbm.1, bf16[1,128,1792]{2,1,0:T(8,128)(2,1)} %cot_hbm.1, bf16[128,896]{1,0:T(8,128)(2,1)} %w_hbm.1, bf16[8,3584]{1,0:T(8,128)(2,1)} %ad_hbm.1, ...), custom_call_target="tpu_custom_call" | custom-call | tf_op jit(solution)/shard_map/pallas_call | solution.py:376
  23.5 2.1 %shard_map.130 = (bf16[1,256,1792]{2,1,0:T(8,128)(2,1)}, f32[32,896]{1,0:T(8,128)}, f32[8,896]{1,0:T(8,128)}, f32[8,448]{1,0:T(8,128)}) custom-call(bf16[1,256,1792]{2,1,0:T(8,128)(2,1)} %get-tuple-element.6.out_hbm, bf16[2,4,3,16,128]{4,3,2,1,0:T(8,128)(2,1)} %get-tuple-element.7.all_hbm), custom_call_target="tpu_custom_call" | custom-call | tf_op jit(solution)/shard_map/pallas_call | solution.py:402

commit v5 on v4

--- a/solution.py
+++ b/solution.py
@@ -18,7 +18,7 @@
 PIECES = 4
 EARLY_PAIRS = 2
 PAIR_GROUP = 3
-STAGES = (1, 13, 22)
+STAGES = (12, 24)
 LOG2E = 1.4426950408889634
 BF16 = jnp.bfloat16
 F32 = jnp.float32
@@ -268,6 +268,8 @@
                 copy.start()
                 pending.append(copy)
 
+    plane_stage()
+
     for copy in kv_copies[:2 * (n_seq - 1)]:
         copy.wait_recv()
     loads[9].wait()
@@ -285,7 +287,7 @@
     heads = tq_ref.shape[1] // HEAD_SIZE
     group = heads // (k_ref.shape[2] // HEAD_SIZE)
     factor = HEAD_SIZE ** (-0.5) * LOG2E
-    stages = dict(zip(STAGES, (plane_stage, dp_stage, gather_stage)))
+    stages = dict(zip(STAGES, (dp_stage, gather_stage)))
     ones_v = jnp.ones((n_seq * keys, HEAD_SIZE), BF16)
     outs = []
 

time: 25.8 us -> 24.9 us (0.965)
  Pallas kernels: 25 us -> 24.1 us
    pallas_call x1, Pallas kernels: 22.8 us -> 21.9 us  [on_device(): pl.pallas_call(functools.partial(kernel, plan), out_shape=(shapes[0], jax...]
where the time goes in v5:
time: 24.9 us; the launch traced here: 24.7 us
  Pallas kernels  24.1 us (97%)
  between operations  0.64 us (3%)
    pallas_call x1, Pallas kernels, on_device(): pl.pallas_call(functools.partial(kernel, plan), out_shape=(shapes[0], jax...  21.9 us
    pallas_call x1, Pallas kernels, on_device(): pl.pallas_call(functools.partial(write_out, plan), out_shape=shapes, in_s...  2.14 us

profile of v5, /device:TPU:0, one launch (start us, length us, event | category | flops | bytes accessed | tf_op | source)
XLA Modules:
  0.0 24.7 jit_solution(7978578356689044299)
XLA Ops:
  0.6 21.9 %shard_map.129 = (bf16[1,256,1792]{2,1,0:T(8,128)(2,1)}, bf16[2,4,3,16,128]{4,3,2,1,0:T(8,128)(2,1)}) custom-call(bf16[1,128,3584]{2,1,0:T(8,128)(2,1)} %x_hbm.1, bf16[1,128,1792]{2,1,0:T(8,128)(2,1)} %sq_hbm.1, bf16[1,128,1792]{2,1,0:T(8,128)(2,1)} %cot_hbm.1, bf16[128,896]{1,0:T(8,128)(2,1)} %w_hbm.1, bf16[8,3584]{1,0:T(8,128)(2,1)} %ad_hbm.1, ...), custom_call_target="tpu_custom_call" | custom-call | tf_op jit(solution)/shard_map/pallas_call | solution.py:378
  22.6 2.1 %shard_map.130 = (bf16[1,256,1792]{2,1,0:T(8,128)(2,1)}, f32[32,896]{1,0:T(8,128)}, f32[8,896]{1,0:T(8,128)}, f32[8,448]{1,0:T(8,128)}) custom-call(bf16[1,256,1792]{2,1,0:T(8,128)(2,1)} %get-tuple-element.6.out_hbm, bf16[2,4,3,16,128]{4,3,2,1,0:T(8,128)(2,1)} %get-tuple-element.7.all_hbm), custom_call_target="tpu_custom_call" | custom-call | tf_op jit(solution)/shard_map/pallas_call | solution.py:404
